TPU v7x, 32 devices: a whole 2x2x4 slice. The times are simulated.
32 devices in a mesh: freq: 8 (over z, x), kgrp: 4 (over y, core).
Axes of the slice: x: 2, y: 2, z: 4, core: 2. Of those that a mesh axis runs over, the one named last changes fastest.
Arguments:
- hamiltonian: float32 [256, 64, 128], P(('freq', 'kgrp')), may hold values from -1 to 1, as said below
- self_energy: float32 [16, 64, 128], P('freq'), may hold values from -0.8 to 0.3, as said below
- guess_factor: float32 [16, 64, 128], P('freq'), may hold values from -0.05 to 1.25
- weights: int32 [256], replicated, may hold values from 1 to 48
- counts: int32 [16], replicated, may hold values from 1 to 3, as said below
Outputs:
- local_green: float32 [4096, 32], P(('freq', 'kgrp'))
Inputs may be any that keep to these rules, and one draw needn't show every extreme that they name: `hamiltonian`: each k-point's matrix is Hermitian: the left half symmetric, the right half antisymmetric. `self_energy`: the diagonal of the right half lies between -0.8 and -0.4. `counts`: the number of Newton-Schulz steps taken at each frequency.
All inputs are finite; a program needn't handle non-finite values.
Results may differ from a plain program's by a relative error of at most 0.0001.
Values sent between devices are 32-bit elements.
A program may use at most 64 MiB of HBM per device.

v0:
```python
import math
import jax
import jax.numpy as jnp
from jax import lax
from jax.sharding import PartitionSpec as P

chem_potential = 0.2


def blockify(right_side):
    order = right_side.shape[-1] // 2
    real_part = right_side[..., :order]
    imag_part = right_side[..., order:]
    upper_row = jnp.concatenate([real_part, imag_part], -1)
    lower_row = jnp.concatenate([-imag_part, real_part], -1)
    return jnp.concatenate([upper_row, lower_row], -2)


def complex_product(left_side, right_side):
    return jnp.einsum(
        "...ij,...jl->...il", left_side, blockify(right_side), precision=lax.Precision.HIGHEST
    )


def build_matrix(kpoint_rows, sigma_rows, matsubara):
    orbitals = kpoint_rows.shape[1]
    identity = jnp.eye(orbitals, dtype=jnp.float32)
    real_shift = jnp.broadcast_to(chem_potential * identity, matsubara.shape + identity.shape)
    imag_shift = matsubara[:, None, None] * identity
    diagonal_shift = jnp.concatenate([real_shift, imag_shift], -1)
    return diagonal_shift[:, None] - kpoint_rows[None] - sigma_rows[:, None]


def start_guess(matrix, factor_rows):
    orbitals = matrix.shape[-2]
    diag_real = jnp.diagonal(matrix[..., :orbitals], axis1=-2, axis2=-1)
    diag_imag = jnp.diagonal(matrix[..., orbitals:], axis1=-2, axis2=-1)
    modulus = diag_real * diag_real + diag_imag * diag_imag
    recip_real = (diag_real / modulus)[..., None]
    recip_imag = (-diag_imag / modulus)[..., None]
    factor_real = factor_rows[..., :orbitals]
    factor_imag = factor_rows[..., orbitals:]
    guess_real = recip_real * factor_real - recip_imag * factor_imag
    guess_imag = recip_real * factor_imag + recip_imag * factor_real
    return jnp.concatenate([guess_real, guess_imag], -1)


def invert_blocks(kpoint_rows, sigma_rows, factor_rows, freq_ids, freq_total, step_counts):
    orbitals = kpoint_rows.shape[1]
    matsubara = (2 * freq_ids + 1).astype(jnp.float32) * (math.pi / (2 * freq_total))
    matrix = build_matrix(kpoint_rows, sigma_rows, matsubara)
    initial = start_guess(matrix, factor_rows[:, None])
    identity = jnp.eye(orbitals, dtype=jnp.float32)
    doubled = jnp.concatenate([2.0 * identity, jnp.zeros_like(identity)], -1)
    longest = jnp.max(step_counts)

    def newton_step(sweep, current):
        updated = complex_product(current, doubled - complex_product(matrix, current))
        active = (sweep < step_counts)[:, None, None, None]
        return jnp.where(active, updated, current)

    return lax.fori_loop(0, longest, newton_step, initial)


def per_device(hamiltonian, self_energy, guess_factor, weights, counts):
    orbitals = hamiltonian.shape[1]
    per_freq = self_energy.shape[0]
    k_local = hamiltonian.shape[0]
    freq_devs = lax.axis_size("freq")
    group_devs = lax.axis_size("kgrp")
    freq_total = per_freq * freq_devs
    pair_block = orbitals * orbitals // (freq_devs * group_devs)
    freq_pos = lax.axis_index("freq")
    group_pos = lax.axis_index("kgrp")
    weight_total = jnp.sum(weights.astype(jnp.float32))
    first_freq = freq_pos * per_freq
    freq_ids = first_freq + jnp.arange(per_freq, dtype=jnp.int32)
    local_counts = lax.dynamic_slice_in_dim(counts, first_freq, per_freq)
    empty = jnp.zeros((per_freq, orbitals, 2 * orbitals), jnp.float32)
    h_piece = lax.all_gather(hamiltonian, "freq", axis=0, tiled=True)
    row_ids = jnp.arange(h_piece.shape[0], dtype=jnp.int32)
    kpoint_ids = (
        row_ids // k_local * (group_devs * k_local) + group_pos * k_local + row_ids % k_local
    )
    factors = jnp.take(weights, kpoint_ids).astype(jnp.float32)
    inverses = invert_blocks(h_piece, self_energy, guess_factor, freq_ids, freq_total, local_counts)
    partial_sum = empty + jnp.einsum(
        "k,fkij->fij", factors, inverses, precision=lax.Precision.HIGHEST
    )
    partial_term = partial_sum.reshape(per_freq, orbitals, 2, orbitals).transpose(0, 2, 1, 3)
    partial_term = partial_term.reshape(per_freq, 2, freq_devs, group_devs, pair_block)
    quarter = lax.psum_scatter(partial_term, "kgrp", scatter_dimension=3, tiled=True)
    own_block = lax.all_to_all(quarter, "freq", split_axis=2, concat_axis=0, tiled=True)
    result = own_block.reshape(freq_total, 2, pair_block).transpose(2, 1, 0)
    result = result.reshape(pair_block, 2 * freq_total)
    return result / weight_total


def solution(mesh):
    return jax.shard_map(
        per_device,
        mesh=mesh,
        in_specs=(
            P(("freq", "kgrp"), None, None),
            P("freq", None, None),
            P("freq", None, None),
            P(),
            P(),
        ),
        out_specs=P(("freq", "kgrp"), None),
        check_vma=False,
    )
```

profile of v0, /device:TPU:0, one launch (start us, length us, event | category | flops | bytes accessed | tf_op | source)
XLA Modules:
  0.0 254.6 jit_solution(18190789245727477502)
XLA Ops:
  7.6 2.6 %copy.25 = f32[2,64,128]{0,2,1:T(8,128)} copy(f32[2,64,128]{2,1,0:T(8,128)S(1)} %pad_maximum_fusion.1) | data formatting | bytes 131072 | tf_op jit(solution)/shard_map/concatenate | solution.py:30
  10.2 2.6 %copy.27 = f32[2,64,128]{0,2,1:T(8,128)} copy(f32[2,64,128]{2,1,0:T(8,128)S(1)} %copy-done.2) | data formatting | bytes 131072 | tf_op args[1]
  14.5 46.8 %all-gather.2.cloned.1.call-done = f32[64,64,128]{2,1,0:T(8,128)} async-done(((f32[8,64,128]{2,1,0:T(8,128)}), f32[64,64,128]{2,1,0:T(8,128)}) %all-gather.2.cloned.1.call-update) | async-done | bytes 2097168 | tf_op jit(solution)/shard_map/all_gather | solution.py:80
  61.3 3.8 %copy.26 = f32[64,64,128]{0,2,1:T(8,128)} copy(f32[64,64,128]{2,1,0:T(8,128)} %all-gather.2.cloned.1.call-done) | data formatting | bytes 4194304 | tf_op jit(solution)/shard_map/all_gather | solution.py:80
  65.1 22.3 %subtract_subtract_fusion = f32[2,64,64,128]{1,0,3,2:T(2,128)} fusion(f32[2,64,128]{0,2,1:T(8,128)} %copy.27, f32[64,64,128]{0,2,1:T(8,128)} %copy.26, f32[2,64,128]{0,2,1:T(8,128)} %copy.25), kind=kLoop, calls=%fused_computation.30 | loop fusion | flops 2097152 | bytes 6422528 | tf_op jit(solution)/shard_map/sub | solution.py:31
  87.4 7.8 %fusion.64 = (f32[2,64,64,64]{1,0,3,2:T(2,128)}, f32[2,64,64,64]{1,0,3,2:T(2,128)}) fusion(f32[2,64,64,128]{1,0,3,2:T(2,128)} %subtract_subtract_fusion), kind=kLoop, calls=%fused_computation.96 | loop fusion | bytes 8388608 | tf_op jit(solution)/shard_map/slice | solution.py:36
  95.3 2.9 %gather_fusion.1 = f32[64,2,64]{2,1,0:T(2,128)S(1)} fusion(f32[2,64,64,64]{1,0,3,2:T(2,128)} %get-tuple-element.83, s32[64]{0:T(128)S(1)} %or_bitcast_fusion), kind=kCustom, calls=%fused_computation.1 | custom fusion | bytes 66048 | tf_op jit(solution)/shard_map/jit(diagonal)/gather | solution.py:36
  98.3 3.0 %gather_fusion.2 = f32[64,2,64]{2,1,0:T(2,128)S(1)} fusion(f32[2,64,64,64]{1,0,3,2:T(2,128)} %get-tuple-element.84, s32[64]{0:T(128)S(1)} %or_bitcast_fusion), kind=kCustom, calls=%fused_computation.2 | custom fusion | bytes 66048 | tf_op jit(solution)/shard_map/jit(diagonal)/gather | solution.py:37
  103.7 3.1 %pad_maximum_fusion = f32[2,64,64,128]{3,2,1,0:T(8,128)} fusion(f32[2,64,64,64]{3,2,1,0:T(8,128)S(1)} %get-tuple-element.86, f32[2,64,64,64]{3,2,1,0:T(8,128)S(1)} %get-tuple-element.85), kind=kLoop, calls=%fused_computation.31 | loop fusion | flops 1048576 | bytes 8388608 | tf_op jit(solution)/shard_map/concatenate | solution.py:45
  106.8 87.1 %while.11 = (s32[]{:T(128)}, f32[2,64,64,128]{3,2,1,0:T(8,128)}, s32[]{:T(128)}, s32[2]{0:T(128)S(1)}, f32[64,128]{1,0:T(8,128)S(1)}, /*index=5*/f32[64,64,128]{...) while((s32[]{:T(128)}, f32[2,64,64,128]{3,2,1,0:T(8,128)}, ...), condition=%wide.region_2.3_spmd.clone, body=%wide.region_1.2_spmd.clone.sunk | while | flops 3234856960 | bytes 56787048 | solution.py:62
  111.3 8.9 %bitcast_subtract_fusion.2 = f32[2,64,64,128]{3,2,1,0:T(8,128)S(1)} fusion(f32[64,128]{1,0:T(8,128)S(1)} %get-tuple-element.171, f32[2,64,128]{2,1,0:T(8,128)S(1)} %get-tuple-element.174, f32[64,64,128]{2,1,0:T(8,128)S(1)} %get-tuple-element.172, f32[2,64,128]{2,1,0:T(8,128)S(1)} %get-tuple-element.173, ...), kind=kOutput, calls=%fused_computation.18.clone.1 | convolution fusion | flops 1617952768 | bytes 14843904 | tf_op jit(solution)/shard_map/while/body/...ij,...jl->...il/dot_general | solution.py:20
  120.2 3.5 %slice_negate_fusion.5 = (f32[2,64,64,64]{3,2,1,0:T(8,128)S(1)}, f32[2,64,64,64]{3,2,1,0:T(8,128)}) fusion(f32[2,64,64,128]{3,2,1,0:T(8,128)S(1)} %bitcast_subtract_fusion.2), kind=kLoop, calls=%fused_computation.16.clone.1 | loop fusion | flops 524288 | bytes 8388608 | tf_op jit(solution)/shard_map/while/body/neg | solution.py:15
  123.7 11.9 %bitcast_select_fusion.2 = f32[2,64,64,128]{3,2,1,0:T(8,128)} fusion(f32[2,64,64,128]{3,2,1,0:T(8,128)S(1)} %copy.51, f32[2,64,64,64]{3,2,1,0:T(8,128)} %get-tuple-element.147, f32[2,64,64,64]{3,2,1,0:T(8,128)S(1)} %get-tuple-element.148, f32[2,64,64,128]{3,2,1,0:T(8,128)S(1)} %bitcast_subtract_fusion.2, pred[2]{0:T(512)(128)(4,1)S(1)} %broadcast_compare_fusion.2), kind=kOutput, calls=%fused_computation.17.clone.1 | convolution fusion | flops 1615855616 | bytes 16777218 | tf_op jit(solution)/shard_map/while/body/...ij,...jl->...il/dot_general | solution.py:20
  139.9 8.9 %bitcast_subtract_fusion.2 = f32[2,64,64,128]{3,2,1,0:T(8,128)S(1)} fusion(f32[64,128]{1,0:T(8,128)S(1)} %get-tuple-element.171, f32[2,64,128]{2,1,0:T(8,128)S(1)} %get-tuple-element.174, f32[64,64,128]{2,1,0:T(8,128)S(1)} %get-tuple-element.172, f32[2,64,128]{2,1,0:T(8,128)S(1)} %get-tuple-element.173, ...), kind=kOutput, calls=%fused_computation.18.clone.1 | convolution fusion | flops 1617952768 | bytes 14843904 | tf_op jit(solution)/shard_map/while/body/...ij,...jl->...il/dot_general | solution.py:20
  148.9 3.5 %slice_negate_fusion.5 = (f32[2,64,64,64]{3,2,1,0:T(8,128)S(1)}, f32[2,64,64,64]{3,2,1,0:T(8,128)}) fusion(f32[2,64,64,128]{3,2,1,0:T(8,128)S(1)} %bitcast_subtract_fusion.2), kind=kLoop, calls=%fused_computation.16.clone.1 | loop fusion | flops 524288 | bytes 8388608 | tf_op jit(solution)/shard_map/while/body/neg | solution.py:15
  152.4 11.9 %bitcast_select_fusion.2 = f32[2,64,64,128]{3,2,1,0:T(8,128)} fusion(f32[2,64,64,128]{3,2,1,0:T(8,128)S(1)} %copy.51, f32[2,64,64,64]{3,2,1,0:T(8,128)} %get-tuple-element.147, f32[2,64,64,64]{3,2,1,0:T(8,128)S(1)} %get-tuple-element.148, f32[2,64,64,128]{3,2,1,0:T(8,128)S(1)} %bitcast_subtract_fusion.2, pred[2]{0:T(512)(128)(4,1)S(1)} %broadcast_compare_fusion.2), kind=kOutput, calls=%fused_computation.17.clone.1 | convolution fusion | flops 1615855616 | bytes 16777218 | tf_op jit(solution)/shard_map/while/body/...ij,...jl->...il/dot_general | solution.py:20
  168.6 8.9 %bitcast_subtract_fusion.2 = f32[2,64,64,128]{3,2,1,0:T(8,128)S(1)} fusion(f32[64,128]{1,0:T(8,128)S(1)} %get-tuple-element.171, f32[2,64,128]{2,1,0:T(8,128)S(1)} %get-tuple-element.174, f32[64,64,128]{2,1,0:T(8,128)S(1)} %get-tuple-element.172, f32[2,64,128]{2,1,0:T(8,128)S(1)} %get-tuple-element.173, ...), kind=kOutput, calls=%fused_computation.18.clone.1 | convolution fusion | flops 1617952768 | bytes 14843904 | tf_op jit(solution)/shard_map/while/body/...ij,...jl->...il/dot_general | solution.py:20
  177.6 3.5 %slice_negate_fusion.5 = (f32[2,64,64,64]{3,2,1,0:T(8,128)S(1)}, f32[2,64,64,64]{3,2,1,0:T(8,128)}) fusion(f32[2,64,64,128]{3,2,1,0:T(8,128)S(1)} %bitcast_subtract_fusion.2), kind=kLoop, calls=%fused_computation.16.clone.1 | loop fusion | flops 524288 | bytes 8388608 | tf_op jit(solution)/shard_map/while/body/neg | solution.py:15
  181.1 11.9 %bitcast_select_fusion.2 = f32[2,64,64,128]{3,2,1,0:T(8,128)} fusion(f32[2,64,64,128]{3,2,1,0:T(8,128)S(1)} %copy.51, f32[2,64,64,64]{3,2,1,0:T(8,128)} %get-tuple-element.147, f32[2,64,64,64]{3,2,1,0:T(8,128)S(1)} %get-tuple-element.148, f32[2,64,64,128]{3,2,1,0:T(8,128)S(1)} %bitcast_subtract_fusion.2, pred[2]{0:T(512)(128)(4,1)S(1)} %broadcast_compare_fusion.2), kind=kOutput, calls=%fused_computation.17.clone.1 | convolution fusion | flops 1615855616 | bytes 16777218 | tf_op jit(solution)/shard_map/while/body/...ij,...jl->...il/dot_general | solution.py:20
  193.9 9.2 %dot_general.18 = f32[2,64,2,64,64]{3,2,1,4,0:T(2,128)} reshape(f32[2,64,128,64]{2,1,3,0:T(8,128)} %bitcast.62) | data formatting | bytes 8388608 | tf_op jit(solution)/shard_map/k,fkij->fij/dot_general | solution.py:87
  203.1 12.3 %fusion.27 = f32[1,2,64,2,64]{4,0,3,2,1:T(1,128)S(1)} fusion(f32[2,64,2,64,64]{3,2,1,4,0:T(2,128)} %dot_general.18, s32[64]{0:T(128)S(1)} %gather_fusion, s32[]{:T(128)S(6)} %mul.134), kind=kOutput, calls=%fused_computation.28 | convolution fusion | flops 12584384 | bytes 4260100 | tf_op jit(solution)/shard_map/k,fkij->fij/dot_general | solution.py:87
  216.1 16.9 %reduce-scatter.2.cloned.1.call-done = f32[2,2,8,1,128]{4,2,1,0,3:T(8,128)} async-done(((f32[2,2,8,4,128]{4,2,1,0,3:T(8,128)}), f32[2,2,8,1,128]{4,2,1,0,3:T(8,128)}) %reduce-scatter.2.cloned.1.call-update) | async-done | bytes 16400 | tf_op jit(solution)/shard_map/reduce_scatter | solution.py:92
  234.4 5.5 %all-to-all-start = ((f32[2,2,8,1,128]{4,3,1,0,2:T(1,128)}), f32[2,2,8,1,128]{4,3,1,0,2:T(1,128)S(1)}, u32[]{:S(2)}, u32[]{:S(2)}) async-start(f32[2,2,8,1,128]{4,3,1,0,2:T(1,128)} %copy.33), calls=%async_computation.1 | async-start | bytes 32768 | tf_op jit(solution)/shard_map/all_to_all | solution.py:93
  240.5 6.0 %all-to-all-done = f32[2,2,8,1,128]{4,3,1,0,2:T(1,128)S(1)} async-done(((f32[2,2,8,1,128]{4,3,1,0,2:T(1,128)}), f32[2,2,8,1,128]{4,3,1,0,2:T(1,128)S(1)}, u32[]{:S(2)}, u32[]{:S(2)}) %all-to-all-start) | async-done | bytes 16416 | tf_op jit(solution)/shard_map/all_to_all | solution.py:93
  (48 shorter events, 19.9 us)
Async XLA Ops:
  6.5 3.6 %copy-start.2 = (f32[2,64,128]{2,1,0:T(8,128)S(1)}, f32[2,64,128]{2,1,0:T(8,128)}, u32[]{:S(2)}) copy-start(f32[2,64,128]{2,1,0:T(8,128)} %param.8) | copy-start | bytes 196612
  6.5 54.8 %all-gather.2.cloned.1.call-start = ((), (), s32[]{:S(2)}) async-start(), calls=%async_computation.2 | async-start | bytes 2359296 | tf_op jit(solution)/shard_map/all_gather | solution.py:80
  7.3 225.8 %reduce-scatter.2.cloned.1.call-start = ((), (), s32[]{:S(2)}) async-start(), calls=%async_computation.3 | async-start | bytes 81920 | tf_op jit(solution)/shard_map/reduce_scatter | solution.py:92
  7.5 5.3 %copy-start = (s32[256]{0:T(256)S(1)}, s32[256]{0:T(256)}, u32[]{:S(2)}) copy-start(s32[256]{0:T(256)} %param.10) | copy-start | bytes 3076
  7.5 6.1 %copy-start.4 = (s32[16]{0:T(128)S(1)}, s32[16]{0:T(128)}, u32[]{:S(2)}) copy-start(s32[16]{0:T(128)} %param.11) | copy-start | bytes 196
  7.6 6.8 %copy-start.3 = (f32[2,64,128]{2,1,0:T(8,128)S(1)}, f32[2,64,128]{2,1,0:T(8,128)}, u32[]{:S(2)}) copy-start(f32[2,64,128]{2,1,0:T(8,128)} %param.9) | copy-start | bytes 196612
  103.7 3.1 %copy-start.1 = (f32[64,64,128]{2,1,0:T(8,128)S(1)}, f32[64,64,128]{2,1,0:T(8,128)}, u32[]{:S(2)}) copy-start(f32[64,64,128]{2,1,0:T(8,128)} %all-gather.2.cloned.1.call-done) | copy-start | bytes 6291460
  234.4 12.1 %all-to-all-start = ((f32[2,2,8,1,128]{4,3,1,0,2:T(1,128)}), f32[2,2,8,1,128]{4,3,1,0,2:T(1,128)S(1)}, u32[]{:S(2)}, u32[]{:S(2)}) async-start(f32[2,2,8,1,128]{4,3,1,0,2:T(1,128)} %copy.33), calls=%async_computation.1 | async-start | bytes 32768 | tf_op jit(solution)/shard_map/all_to_all | solution.py:93
Sparse Core Ops, SparseCore 0:
  9.5 51.7 all-gather.1
  216.2 16.7 reduce-scatter.1
where the time goes:
time: 255 us
  matrix products  74.9 us (29%)
  waiting for transfers between devices  70.5 us (28%)
  other arithmetic  44.8 us (18%)
  local copies, waits for them, and re-layouts  42.3 us (17%)
  between operations  13.6 us (5%)
  starting transfers between devices  5.57 us (2%)
  loops' own time  3.03 us (1%)
    dot_general x6, matrix products, complex_product(): jnp.einsum('...ij,...jl->...il', left_side, blockify(right_side), precisi...  62.6 us
    all_gather x1, waiting for transfers between devices, per_device(): h_piece = lax.all_gather(hamiltonian, 'freq', axis=0, tiled=True)  46.8 us
    sub x1, other arithmetic, build_matrix(): return diagonal_shift[:, None] - kpoint_rows[None] - sigma_rows[:, None]  22.3 us
    reduce_scatter x1, waiting for transfers between devices, per_device(): lax.psum_scatter(partial_term, 'kgrp', scatter_dimension=3, tiled=True)  16.9 us
    neg x6, other arithmetic, blockify(): lower_row = jnp.concatenate([-imag_part, real_part], -1)  14.8 us
    dot_general x1, matrix products, per_device(): jnp.einsum('k,fkij->fij', factors, inverses, precision=lax.Precision.HIGH...  12.3 us
    dot_general x2, local copies, waits for them, and re-layouts, per_device(): jnp.einsum('k,fkij->fij', factors, inverses, precision=lax.Precision.HIGH...  9.2 us
    slice x1, local copies, waits for them, and re-layouts, start_guess(): diag_real = jnp.diagonal(matrix[..., :orbitals], axis1=-2, axis2=-1)  7.83 us
  transfers between devices with their start and end apart: 3, of which 3 were waited for; matrix products, arithmetic and copies ran while one was open for 3% of the time, Pallas kernels for 0%

commit v1 on v0

--- a/solution.py
+++ b/solution.py
@@ -5,6 +5,18 @@
 from jax.sharding import PartitionSpec as P
 
 chem_potential = 0.2
+
+
+def ring_gather(shard, axis, dim):
+    ways, here, hop = (lax.axis_size(axis), lax.axis_index(axis), shard.shape[dim])
+    shape = [n * ways if d == dim else n for d, n in enumerate(shard.shape)]
+    full = lax.dynamic_update_slice_in_dim(
+        jnp.zeros(shape, shard.dtype), shard, here * hop, axis=dim
+    )
+    for far in range(1, ways):
+        shard = lax.ppermute(shard, axis, [(d, (d + 1) % ways) for d in range(ways)])
+        full = lax.dynamic_update_slice_in_dim(full, shard, (here - far) % ways * hop, axis=dim)
+    return full
 
 
 def blockify(right_side):
@@ -77,7 +89,7 @@
     freq_ids = first_freq + jnp.arange(per_freq, dtype=jnp.int32)
     local_counts = lax.dynamic_slice_in_dim(counts, first_freq, per_freq)
     empty = jnp.zeros((per_freq, orbitals, 2 * orbitals), jnp.float32)
-    h_piece = lax.all_gather(hamiltonian, "freq", axis=0, tiled=True)
+    h_piece = ring_gather(hamiltonian, "freq", 0)
     row_ids = jnp.arange(h_piece.shape[0], dtype=jnp.int32)
     kpoint_ids = (
         row_ids // k_local * (group_devs * k_local) + group_pos * k_local + row_ids % k_local

time: 255 us -> 269 us (1.055)
  waiting for transfers between devices: 70.5 us -> 78.9 us
  starting transfers between devices: 5.57 us -> 8.47 us
    ppermute x0 -> x7, waiting for transfers between devices: none -> 56.1 us  [ring_gather(): lax.ppermute(shard, axis, [(d, (d + 1) % ways) for d in range(ways)])]
    all_gather x1 -> x0, waiting for transfers between devices: 46.8 us -> none  [per_device(): h_piece = lax.all_gather(hamiltonian, 'freq', axis=0, tiled=True)]
    dynamic_update_slice x0 -> x9, local copies, waits for them, and re-layouts: none -> 4.83 us  [the longest x8 3.85 us: ring_gather(): lax.dynamic_update_slice_in_dim(full, shard, (here - far) % ways * hop, a...]
    all_gather x1 -> x0, local copies, waits for them, and re-layouts: 3.82 us -> none  [per_device(): h_piece = lax.all_gather(hamiltonian, 'freq', axis=0, tiled=True)]
    ppermute x0 -> x7, starting transfers between devices: none -> 2.98 us  [ring_gather(): lax.ppermute(shard, axis, [(d, (d + 1) % ways) for d in range(ways)])]
  transfers between devices with their start and end apart: 3 -> 9, of which waited for: 3 -> 9; matrix products, arithmetic and copies ran while one was open for 3% -> 4% of each run, Pallas kernels for 0% -> 0%
where the time goes in v1:
time: 269 us; the launch traced here: 268 us
  waiting for transfers between devices  78.9 us (29%)
  matrix products  75.1 us (28%)
  other arithmetic  45.5 us (17%)
  local copies, waits for them, and re-layouts  43.5 us (16%)
  between operations  13.6 us (5%)
  starting transfers between devices  8.47 us (3%)
  loops' own time  3.24 us (1%)
    dot_general x6, matrix products, complex_product(): jnp.einsum('...ij,...jl->...il', left_side, blockify(right_side), precisi...  62.8 us
    ppermute x7, waiting for transfers between devices, ring_gather(): lax.ppermute(shard, axis, [(d, (d + 1) % ways) for d in range(ways)])  56.1 us
    sub x1, other arithmetic, build_matrix(): return diagonal_shift[:, None] - kpoint_rows[None] - sigma_rows[:, None]  22.3 us
    reduce_scatter x1, waiting for transfers between devices, per_device(): lax.psum_scatter(partial_term, 'kgrp', scatter_dimension=3, tiled=True)  16.8 us
    neg x6, other arithmetic, blockify(): lower_row = jnp.concatenate([-imag_part, real_part], -1)  14.8 us
    dot_general x1, matrix products, per_device(): jnp.einsum('k,fkij->fij', factors, inverses, precision=lax.Precision.HIGH...  12.3 us
    dot_general x2, local copies, waits for them, and re-layouts, per_device(): jnp.einsum('k,fkij->fij', factors, inverses, precision=lax.Precision.HIGH...  9.2 us
    slice x1, local copies, waits for them, and re-layouts, start_guess(): diag_real = jnp.diagonal(matrix[..., :orbitals], axis1=-2, axis2=-1)  7.83 us
  transfers between devices with their start and end apart: 9, of which 9 were waited for; matrix products, arithmetic and copies ran while one was open for 4% of the time, Pallas kernels for 0%

profile of v1, /device:TPU:0, one launch (start us, length us, event | category | flops | bytes accessed | tf_op | source)
XLA Modules:
  0.0 268.2 jit_solution(11060126413458793453)
XLA Ops:
  9.5 9.5 %collective-permute-done = f32[8,64,128]{2,1,0:T(8,128)S(1)} collective-permute-done((f32[8,64,128]{2,1,0:T(8,128)}, f32[8,64,128]{2,1,0:T(8,128)S(1)}, u32[]{:S(2)}, u32[]{:S(2)}) %collective-permute-start) | collective-permute-done | bytes 262176 | tf_op jit(solution)/shard_map/ppermute | solution.py:17
  19.1 10.1 %collective-permute-done.1 = f32[8,64,128]{2,1,0:T(8,128)S(1)} collective-permute-done((f32[8,64,128]{2,1,0:T(8,128)S(1)}, f32[8,64,128]{2,1,0:T(8,128)S(1)}, u32[]{:S(2)}, u32[]{:S(2)}) %collective-permute-start.1) | collective-permute-done | bytes 262176 | tf_op jit(solution)/shard_map/ppermute | solution.py:17
  29.3 9.2 %collective-permute-done.2 = f32[8,64,128]{2,1,0:T(8,128)S(1)} collective-permute-done((f32[8,64,128]{2,1,0:T(8,128)S(1)}, f32[8,64,128]{2,1,0:T(8,128)S(1)}, u32[]{:S(2)}, u32[]{:S(2)}) %collective-permute-start.2) | collective-permute-done | bytes 262176 | tf_op jit(solution)/shard_map/ppermute | solution.py:17
  39.9 7.7 %collective-permute-done.3 = f32[8,64,128]{2,1,0:T(8,128)S(1)} collective-permute-done((f32[8,64,128]{2,1,0:T(8,128)S(1)}, f32[8,64,128]{2,1,0:T(8,128)S(1)}, u32[]{:S(2)}, u32[]{:S(2)}) %collective-permute-start.3) | collective-permute-done | bytes 262176 | tf_op jit(solution)/shard_map/ppermute | solution.py:17
  56.9 9.8 %collective-permute-done.5 = f32[8,64,128]{2,1,0:T(8,128)S(1)} collective-permute-done((f32[8,64,128]{2,1,0:T(8,128)}, f32[8,64,128]{2,1,0:T(8,128)S(1)}, u32[]{:S(2)}, u32[]{:S(2)}) %collective-permute-start.5) | collective-permute-done | bytes 262176 | tf_op jit(solution)/shard_map/ppermute | solution.py:17
  67.7 8.0 %collective-permute-done.6 = f32[8,64,128]{2,1,0:T(8,128)S(1)} collective-permute-done((f32[8,64,128]{2,1,0:T(8,128)S(1)}, f32[8,64,128]{2,1,0:T(8,128)S(1)}, u32[]{:S(2)}, u32[]{:S(2)}) %collective-permute-start.6) | collective-permute-done | bytes 262176 | tf_op jit(solution)/shard_map/ppermute | solution.py:17
  78.5 22.3 %subtract_subtract_fusion = f32[2,64,64,128]{1,0,3,2:T(2,128)} fusion(f32[2,64,128]{0,2,1:T(8,128)} %copy.27, f32[64,64,128]{0,2,1:T(8,128)} %copy.26, f32[2,64,128]{0,2,1:T(8,128)} %copy.25), kind=kLoop, calls=%fused_computation.30 | loop fusion | flops 2097152 | bytes 6422528 | tf_op jit(solution)/shard_map/sub | solution.py:43
  100.8 7.8 %fusion.63 = (f32[2,64,64,64]{1,0,3,2:T(2,128)}, f32[2,64,64,64]{1,0,3,2:T(2,128)}) fusion(f32[2,64,64,128]{1,0,3,2:T(2,128)} %subtract_subtract_fusion), kind=kLoop, calls=%fused_computation.103 | loop fusion | bytes 8388608 | tf_op jit(solution)/shard_map/slice | solution.py:48
  117.1 3.1 %pad_maximum_fusion = f32[2,64,64,128]{3,2,1,0:T(8,128)} fusion(f32[2,64,64,64]{3,2,1,0:T(8,128)S(1)} %get-tuple-element.86, f32[2,64,64,64]{3,2,1,0:T(8,128)S(1)} %get-tuple-element.85), kind=kLoop, calls=%fused_computation.31 | loop fusion | flops 1048576 | bytes 8388608 | tf_op jit(solution)/shard_map/concatenate | solution.py:57
  120.2 87.5 %while.11 = (s32[]{:T(128)}, f32[2,64,64,128]{3,2,1,0:T(8,128)}, s32[]{:T(128)}, s32[2]{0:T(128)S(1)}, f32[64,128]{1,0:T(8,128)S(1)}, /*index=5*/f32[64,64,128]{...) while((s32[]{:T(128)}, f32[2,64,64,128]{3,2,1,0:T(8,128)}, ...), condition=%wide.region_2.3_spmd.clone, body=%wide.region_1.2_spmd.clone.sunk | while | flops 3234856960 | bytes 56787048 | solution.py:74
  124.7 9.0 %bitcast_subtract_fusion.2 = f32[2,64,64,128]{3,2,1,0:T(8,128)S(1)} fusion(f32[64,128]{1,0:T(8,128)S(1)} %get-tuple-element.173, f32[2,64,128]{2,1,0:T(8,128)S(1)} %get-tuple-element.176, f32[64,64,128]{2,1,0:T(8,128)S(1)} %get-tuple-element.174, f32[2,64,128]{2,1,0:T(8,128)S(1)} %get-tuple-element.175, ...), kind=kOutput, calls=%fused_computation.18.clone.1 | convolution fusion | flops 1617952768 | bytes 14843904 | tf_op jit(solution)/shard_map/while/body/...ij,...jl->...il/dot_general | solution.py:32
  133.7 3.5 %slice_negate_fusion.5 = (f32[2,64,64,64]{3,2,1,0:T(8,128)S(1)}, f32[2,64,64,64]{3,2,1,0:T(8,128)}) fusion(f32[2,64,64,128]{3,2,1,0:T(8,128)S(1)} %bitcast_subtract_fusion.2), kind=kLoop, calls=%fused_computation.16.clone.1 | loop fusion | flops 524288 | bytes 8388608 | tf_op jit(solution)/shard_map/while/body/neg | solution.py:27
  137.2 11.9 %bitcast_select_fusion.2 = f32[2,64,64,128]{3,2,1,0:T(8,128)} fusion(f32[2,64,64,128]{3,2,1,0:T(8,128)S(1)} %copy.59, f32[2,64,64,64]{3,2,1,0:T(8,128)} %get-tuple-element.149, f32[2,64,64,64]{3,2,1,0:T(8,128)S(1)} %get-tuple-element.150, f32[2,64,64,128]{3,2,1,0:T(8,128)S(1)} %bitcast_subtract_fusion.2, pred[2]{0:T(512)(128)(4,1)S(1)} %broadcast_compare_fusion.2), kind=kOutput, calls=%fused_computation.17.clone.1 | convolution fusion | flops 1615855616 | bytes 16777218 | tf_op jit(solution)/shard_map/while/body/...ij,...jl->...il/dot_general | solution.py:32
  153.5 9.0 %bitcast_subtract_fusion.2 = f32[2,64,64,128]{3,2,1,0:T(8,128)S(1)} fusion(f32[64,128]{1,0:T(8,128)S(1)} %get-tuple-element.173, f32[2,64,128]{2,1,0:T(8,128)S(1)} %get-tuple-element.176, f32[64,64,128]{2,1,0:T(8,128)S(1)} %get-tuple-element.174, f32[2,64,128]{2,1,0:T(8,128)S(1)} %get-tuple-element.175, ...), kind=kOutput, calls=%fused_computation.18.clone.1 | convolution fusion | flops 1617952768 | bytes 14843904 | tf_op jit(solution)/shard_map/while/body/...ij,...jl->...il/dot_general | solution.py:32
  162.5 3.5 %slice_negate_fusion.5 = (f32[2,64,64,64]{3,2,1,0:T(8,128)S(1)}, f32[2,64,64,64]{3,2,1,0:T(8,128)}) fusion(f32[2,64,64,128]{3,2,1,0:T(8,128)S(1)} %bitcast_subtract_fusion.2), kind=kLoop, calls=%fused_computation.16.clone.1 | loop fusion | flops 524288 | bytes 8388608 | tf_op jit(solution)/shard_map/while/body/neg | solution.py:27
  166.0 11.9 %bitcast_select_fusion.2 = f32[2,64,64,128]{3,2,1,0:T(8,128)} fusion(f32[2,64,64,128]{3,2,1,0:T(8,128)S(1)} %copy.59, f32[2,64,64,64]{3,2,1,0:T(8,128)} %get-tuple-element.149, f32[2,64,64,64]{3,2,1,0:T(8,128)S(1)} %get-tuple-element.150, f32[2,64,64,128]{3,2,1,0:T(8,128)S(1)} %bitcast_subtract_fusion.2, pred[2]{0:T(512)(128)(4,1)S(1)} %broadcast_compare_fusion.2), kind=kOutput, calls=%fused_computation.17.clone.1 | convolution fusion | flops 1615855616 | bytes 16777218 | tf_op jit(solution)/shard_map/while/body/...ij,...jl->...il/dot_general | solution.py:32
  182.3 9.0 %bitcast_subtract_fusion.2 = f32[2,64,64,128]{3,2,1,0:T(8,128)S(1)} fusion(f32[64,128]{1,0:T(8,128)S(1)} %get-tuple-element.173, f32[2,64,128]{2,1,0:T(8,128)S(1)} %get-tuple-element.176, f32[64,64,128]{2,1,0:T(8,128)S(1)} %get-tuple-element.174, f32[2,64,128]{2,1,0:T(8,128)S(1)} %get-tuple-element.175, ...), kind=kOutput, calls=%fused_computation.18.clone.1 | convolution fusion | flops 1617952768 | bytes 14843904 | tf_op jit(solution)/shard_map/while/body/...ij,...jl->...il/dot_general | solution.py:32
  191.3 3.5 %slice_negate_fusion.5 = (f32[2,64,64,64]{3,2,1,0:T(8,128)S(1)}, f32[2,64,64,64]{3,2,1,0:T(8,128)}) fusion(f32[2,64,64,128]{3,2,1,0:T(8,128)S(1)} %bitcast_subtract_fusion.2), kind=kLoop, calls=%fused_computation.16.clone.1 | loop fusion | flops 524288 | bytes 8388608 | tf_op jit(solution)/shard_map/while/body/neg | solution.py:27
  194.8 11.9 %bitcast_select_fusion.2 = f32[2,64,64,128]{3,2,1,0:T(8,128)} fusion(f32[2,64,64,128]{3,2,1,0:T(8,128)S(1)} %copy.59, f32[2,64,64,64]{3,2,1,0:T(8,128)} %get-tuple-element.149, f32[2,64,64,64]{3,2,1,0:T(8,128)S(1)} %get-tuple-element.150, f32[2,64,64,128]{3,2,1,0:T(8,128)S(1)} %bitcast_subtract_fusion.2, pred[2]{0:T(512)(128)(4,1)S(1)} %broadcast_compare_fusion.2), kind=kOutput, calls=%fused_computation.17.clone.1 | convolution fusion | flops 1615855616 | bytes 16777218 | tf_op jit(solution)/shard_map/while/body/...ij,...jl->...il/dot_general | solution.py:32
  207.7 9.2 %dot_general.18 = f32[2,64,2,64,64]{3,2,1,4,0:T(2,128)} reshape(f32[2,64,128,64]{2,1,3,0:T(8,128)} %bitcast.62) | data formatting | bytes 8388608 | tf_op jit(solution)/shard_map/k,fkij->fij/dot_general | solution.py:99
  216.9 12.3 %fusion.27 = f32[1,2,64,2,64]{4,0,3,2,1:T(1,128)S(1)} fusion(f32[2,64,2,64,64]{3,2,1,4,0:T(2,128)} %dot_general.18, s32[64]{0:T(128)S(1)} %gather_fusion, s32[]{:T(128)S(6)} %mul.158), kind=kOutput, calls=%fused_computation.28 | convolution fusion | flops 12584384 | bytes 4260100 | tf_op jit(solution)/shard_map/k,fkij->fij/dot_general | solution.py:99
  229.9 16.8 %reduce-scatter.2.cloned.1.call-done = f32[2,2,8,1,128]{4,2,1,0,3:T(8,128)} async-done(((f32[2,2,8,4,128]{4,2,1,0,3:T(8,128)}), f32[2,2,8,1,128]{4,2,1,0,3:T(8,128)}) %reduce-scatter.2.cloned.1.call-update) | async-done | bytes 16400 | tf_op jit(solution)/shard_map/reduce_scatter | solution.py:104
  248.1 5.5 %all-to-all-start = ((f32[2,2,8,1,128]{4,3,1,0,2:T(1,128)}), f32[2,2,8,1,128]{4,3,1,0,2:T(1,128)S(1)}, u32[]{:S(2)}, u32[]{:S(2)}) async-start(f32[2,2,8,1,128]{4,3,1,0,2:T(1,128)} %copy.33), calls=%async_computation.1 | async-start | bytes 32768 | tf_op jit(solution)/shard_map/all_to_all | solution.py:105
  254.2 5.9 %all-to-all-done = f32[2,2,8,1,128]{4,3,1,0,2:T(1,128)S(1)} async-done(((f32[2,2,8,1,128]{4,3,1,0,2:T(1,128)}), f32[2,2,8,1,128]{4,3,1,0,2:T(1,128)S(1)}, u32[]{:S(2)}, u32[]{:S(2)}) %all-to-all-start) | async-done | bytes 16416 | tf_op jit(solution)/shard_map/all_to_all | solution.py:105
  (63 shorter events, 40.7 us)
Async XLA Ops:
  6.5 45.1 %copy-start.1 = (f32[2,64,128]{2,1,0:T(8,128)S(1)}, f32[2,64,128]{2,1,0:T(8,128)}, u32[]{:S(2)}) copy-start(f32[2,64,128]{2,1,0:T(8,128)} %param.8) | copy-start | bytes 196612
  6.5 240.2 %reduce-scatter.2.cloned.1.call-start = ((), (), s32[]{:S(2)}) async-start(), calls=%async_computation.2 | async-start | bytes 81920 | tf_op jit(solution)/shard_map/reduce_scatter | solution.py:104
  6.5 12.5 %collective-permute-start = (f32[8,64,128]{2,1,0:T(8,128)}, f32[8,64,128]{2,1,0:T(8,128)S(1)}, u32[]{:S(2)}, u32[]{:S(2)}) collective-permute-start(f32[8,64,128]{2,1,0:T(8,128)} %param.7), channel_id=1, source_target_pairs={{0,4},{4,8},{8,12},{12,16},{16,20},{20,24},{24,28},{28,0},{1,5},{5... | collective-permute-start | bytes 786440 | tf_op jit(solution)/shard_map/ppermute | solution.py:17
  19.1 10.2 %collective-permute-start.1 = (f32[8,64,128]{2,1,0:T(8,128)S(1)}, f32[8,64,128]{2,1,0:T(8,128)S(1)}, u32[]{:S(2)}, u32[]{:S(2)}) collective-permute-start(f32[8,64,128]{2,1,0:T(8,128)S(1)} %collective-permute-done), channel_id=1, source_target_pairs={{0,4},{4,8},{8,12},{12,16},{16,20},{20,24},{24,28},{28,0},{1,5},{5... | collective-permute-start | bytes 786440 | tf_op jit(solution)/shard_map/ppermute | solution.py:17
  29.2 9.3 %collective-permute-start.2 = (f32[8,64,128]{2,1,0:T(8,128)S(1)}, f32[8,64,128]{2,1,0:T(8,128)S(1)}, u32[]{:S(2)}, u32[]{:S(2)}) collective-permute-start(f32[8,64,128]{2,1,0:T(8,128)S(1)} %collective-permute-done.1), channel_id=1, source_target_pairs={{0,4},{4,8},{8,12},{12,16},{16,20},{20,24},{24,28},{28,0},{1,5},{5... | collective-permute-start | bytes 786440 | tf_op jit(solution)/shard_map/ppermute | solution.py:17
  38.5 9.1 %collective-permute-start.3 = (f32[8,64,128]{2,1,0:T(8,128)S(1)}, f32[8,64,128]{2,1,0:T(8,128)S(1)}, u32[]{:S(2)}, u32[]{:S(2)}) collective-permute-start(f32[8,64,128]{2,1,0:T(8,128)S(1)} %collective-permute-done.2), channel_id=1, source_target_pairs={{0,4},{4,8},{8,12},{12,16},{16,20},{20,24},{24,28},{28,0},{1,5},{5... | collective-permute-start | bytes 786440 | tf_op jit(solution)/shard_map/ppermute | solution.py:17
  47.6 9.2 %collective-permute-start.4 = (f32[8,64,128]{2,1,0:T(8,128)S(1)}, f32[8,64,128]{2,1,0:T(8,128)}, u32[]{:S(2)}, u32[]{:S(2)}) collective-permute-start(f32[8,64,128]{2,1,0:T(8,128)S(1)} %collective-permute-done.3), channel_id=1, source_target_pairs={{0,4},{4,8},{8,12},{12,16},{16,20},{20,24},{24,28},{28,0},{1,5},{5... | collective-permute-start | bytes 786440 | tf_op jit(solution)/shard_map/ppermute | solution.py:17
  49.1 5.2 %copy-start = (s32[256]{0:T(256)S(1)}, s32[256]{0:T(256)}, u32[]{:S(2)}) copy-start(s32[256]{0:T(256)} %param.10) | copy-start | bytes 3076
  49.1 6.0 %copy-start.2 = (f32[2,64,128]{2,1,0:T(8,128)S(1)}, f32[2,64,128]{2,1,0:T(8,128)}, u32[]{:S(2)}) copy-start(f32[2,64,128]{2,1,0:T(8,128)} %param.9) | copy-start | bytes 196612
  56.8 9.9 %collective-permute-start.5 = (f32[8,64,128]{2,1,0:T(8,128)}, f32[8,64,128]{2,1,0:T(8,128)S(1)}, u32[]{:S(2)}, u32[]{:S(2)}) collective-permute-start(f32[8,64,128]{2,1,0:T(8,128)} %collective-permute-done.4), channel_id=1, source_target_pairs={{0,4},{4,8},{8,12},{12,16},{16,20},{20,24},{24,28},{28,0},{1,5},{5... | collective-permute-start | bytes 786440 | tf_op jit(solution)/shard_map/ppermute | solution.py:17
  66.7 9.1 %collective-permute-start.6 = (f32[8,64,128]{2,1,0:T(8,128)S(1)}, f32[8,64,128]{2,1,0:T(8,128)S(1)}, u32[]{:S(2)}, u32[]{:S(2)}) collective-permute-start(f32[8,64,128]{2,1,0:T(8,128)S(1)} %collective-permute-done.5), channel_id=1, source_target_pairs={{0,4},{4,8},{8,12},{12,16},{16,20},{20,24},{24,28},{28,0},{1,5},{5... | collective-permute-start | bytes 786440 | tf_op jit(solution)/shard_map/ppermute | solution.py:17
  248.1 12.1 %all-to-all-start = ((f32[2,2,8,1,128]{4,3,1,0,2:T(1,128)}), f32[2,2,8,1,128]{4,3,1,0,2:T(1,128)S(1)}, u32[]{:S(2)}, u32[]{:S(2)}) async-start(f32[2,2,8,1,128]{4,3,1,0,2:T(1,128)} %copy.33), calls=%async_computation.1 | async-start | bytes 32768 | tf_op jit(solution)/shard_map/all_to_all | solution.py:105
Sparse Core Ops, SparseCore 0:
  230.0 16.6 reduce-scatter.1
